TPU v7x, 32 devices: a whole 2x2x4 slice. The times are simulated.
32 devices in a mesh: batch: 4 (over y, x), centre: 8 (over z, core).
Axes of the slice: x: 2, y: 2, z: 4, core: 2. Of those that a mesh axis runs over, the one named last changes fastest.
Arguments:
- pool: float32 [1024, 1024], P('batch', 'centre'), may hold values from -4.5 to 4.5
- sample_index: int32 [512], P('batch'), may hold values from 0 to 255
- targets: float32 [512, 256], P('batch'), may hold values from -6 to 6
- centres: float32 [512, 1024], P(('batch', 'centre')), may hold values from -4.5 to 4.5
- coeffs: float32 [512, 256], P(('batch', 'centre')), may hold values from -6 to 6
- eigvecs: float32 [512, 1024], P(('batch', 'centre')), may hold values from -0.75 to 0.75
- eigscale: float32 [1024], replicated, may hold values from 0.1 to 0.95
Outputs:
- new_coeffs: float32 [512, 256], P(('batch', 'centre'))
Inputs may be any that keep to these rules, and one draw needn't show every extreme that they name: `sample_index`: each batch row's sample lies in the block of 256 training samples held by its own batch group; the index counts within that block.
All inputs are finite; a program needn't handle non-finite values.
Results may differ from a plain program's by a relative error of at most 0.0003.
Values sent between devices are 32-bit elements; how exact they have to be, the bound alone decides.
A program may use at most 64 MiB of HBM per device.

v0:
```python
import jax
import jax.numpy as jnp
from jax import lax
from jax.sharding import PartitionSpec as P


def on_device(pool, sample_index, targets, centres, coeffs, eigvecs, eigscale):
    highest = lax.Precision.HIGHEST
    picked = jnp.take(pool, sample_index, axis=0)
    batch_x = lax.all_gather(picked, "centre", axis=1, tiled=True)
    row_count = batch_x.shape[0]
    n_batch = lax.axis_size("batch")
    n_centre = lax.axis_size("centre")
    own_centres = centres.shape[0]
    group_rows = own_centres * n_batch
    total_centres = group_rows * n_centre
    total_rows = row_count * n_batch
    width = batch_x.shape[1]
    inv_width = 1.0 / jnp.sqrt(jnp.float32(width))
    model_norm = 1.0 / jnp.sqrt(jnp.float32(total_centres))
    zrows = lax.all_gather(centres, "batch", axis=0, tiled=True)
    crows = lax.all_gather(coeffs, "batch", axis=0, tiled=True)
    scores = lax.dot_general(
        batch_x,
        zrows,
        (((1,), (1,)), ((), ())),
        precision=highest,
        preferred_element_type=jnp.float32,
    )
    kpiece = jnp.exp(scores * inv_width)
    partial_value = jnp.dot(kpiece, crows, precision=highest, preferred_element_type=jnp.float32)
    kernel, partial_value = (kpiece, partial_value)
    columns = (
        lax.psum_scatter(partial_value, "centre", scatter_dimension=1, tiled=True) * model_norm
    )
    col_width = columns.shape[1]
    col_offset = lax.axis_index("centre") * col_width
    own_targets = lax.dynamic_slice_in_dim(targets, col_offset, col_width, 1)
    residual = lax.all_gather(columns - own_targets, "centre", axis=1, tiled=True)
    gradient = (
        lax.psum_scatter(
            lax.dot_general(
                kernel,
                residual,
                (((0,), (0,)), ((), ())),
                precision=highest,
                preferred_element_type=jnp.float32,
            ),
            "batch",
            scatter_dimension=0,
            tiled=True,
        )
        * model_norm
    )
    local_coords = lax.dot_general(
        eigvecs,
        gradient,
        (((0,), (0,)), ((), ())),
        precision=highest,
        preferred_element_type=jnp.float32,
    )
    coords = lax.psum(local_coords, ("batch", "centre"))
    correction = jnp.dot(
        eigvecs, eigscale[:, None] * coords, precision=highest, preferred_element_type=jnp.float32
    )
    step_size = 0.5 * jnp.sqrt(jnp.float32(total_centres) / jnp.float32(total_rows))
    return coeffs - step_size * (gradient - correction)


def solution(mesh):
    return jax.shard_map(
        on_device,
        mesh=mesh,
        in_specs=(
            P("batch", "centre"),
            P("batch"),
            P("batch", None),
            P(("batch", "centre"), None),
            P(("batch", "centre"), None),
            P(("batch", "centre"), None),
            P(),
        ),
        out_specs=P(("batch", "centre"), None),
        check_vma=False,
    )
```

profile of v0, /device:TPU:0, one launch (start us, length us, event | category | flops | bytes accessed | tf_op | source)
XLA Modules:
  0.0 257.5 jit_solution(9517945055729336617)
XLA Ops:
  6.5 0.0 copy-start
  6.5 0.0 copy-start.7
  6.5 0.0 copy-start.4
  6.5 0.0 reduce-scatter.7.cloned.1.call-start
  6.5 0.7 compare_and_fusion
  7.3 0.0 copy-done.7
  7.3 9.9 %all_gather.14 = f32[64,256]{1,0:T(8,128)S(1)} all-gather(f32[16,256]{1,0:T(8,128)} %param.11), channel_id=1, replica_groups=mesh['batch'=4,'centre'=8] {'batch'}, dimensions={0}, use_global_device_ids=true | all-gather | bytes 81920 | tf_op jit(solution)/shard_map/all_gather | solution.py:22
  17.2 0.0 copy-done.4
  17.2 8.8 %all_gather.13 = f32[64,1024]{1,0:T(8,128)S(1)} all-gather(f32[16,1024]{1,0:T(8,128)S(1)} %copy-done.4), channel_id=1, replica_groups=mesh['batch'=4,'centre'=8] {'batch'}, dimensions={0}, use_global_device_ids=true | all-gather | bytes 327680 | tf_op jit(solution)/shard_map/all_gather | solution.py:21
  26.0 0.0 copy-done
  26.0 0.6 gather_fusion
  26.6 0.1 broadcast_select_fusion
  26.7 15.2 %all_gather.12 = f32[128,1024]{1,0:T(8,128)S(1)} all-gather(f32[128,128]{1,0:T(8,128)S(1)} %broadcast_select_fusion), channel_id=1, replica_groups=mesh['batch'=4,'centre'=8] {'centre'}, dimensions={1}, use_global_device_ids=true | all-gather | bytes 589824 | tf_op jit(solution)/shard_map/all_gather | solution.py:10
  41.9 0.7 fusion
  42.6 1.1 convolution_bitcast_fusion.1
  43.7 0.0 copy-start.5
  43.7 0.0 reduce-scatter.7.cloned.1.call-update
  43.7 0.0 reduce-scatter.5.cloned.1.call-start
  43.7 0.8 copy-done.5
  44.6 0.1 constant_dynamic-slice_fusion
  44.6 0.1 copy.15
  44.7 29.6 %reduce-scatter.7.cloned.1.call-done = f32[32,128]{1,0:T(8,128)} async-done(((f32[256,128]{1,0:T(8,128)}), f32[32,128]{1,0:T(8,128)}) %reduce-scatter.7.cloned.1.call-update) | async-done | bytes 16400
  74.3 0.7 fusion.6
  75.1 13.9 %all_gather.15 = f32[128,256]{0,1:T(8,128)S(1)} all-gather(f32[128,32]{0,1:T(8,128)S(1)} %fusion.6), channel_id=1, replica_groups=mesh['batch'=4,'centre'=8] {'centre'}, dimensions={1}, use_global_device_ids=true | all-gather | bytes 147456 | tf_op jit(solution)/shard_map/all_gather | solution.py:39
  89.0 0.9 fusion.10
  89.9 0.0 copy-start.1
  89.9 0.0 reduce-scatter.5.cloned.1.call-update
  89.9 0.0 all-reduce.2.cloned.1.call-start
  90.0 22.3 %reduce-scatter.5.cloned.1.call-done = f32[16,256]{1,0:T(8,128)} async-done(((f32[64,256]{1,0:T(8,128)}), f32[16,256]{1,0:T(8,128)}) %reduce-scatter.5.cloned.1.call-update) | async-done | bytes 16400 | tf_op jit(solution)/shard_map/reduce_scatter | solution.py:41
  112.3 0.0 copy-done.1
  112.3 2.8 %convolution_bitcast_fusion = f32[1024,256]{0,1:T(8,128)} fusion(f32[16,1024]{1,0:T(8,128)S(1)} %copy-done.1, f32[16,256]{1,0:T(8,128)} %reduce-scatter.5.cloned.1.call-done), kind=kOutput, calls=%fused_computation.1 | convolution fusion | flops 50335744 | bytes 1130496 | tf_op jit(solution)/shard_map/dot_general | solution.py:55
  115.1 0.0 copy-start.2
  115.1 0.0 copy-start.3
  115.1 0.0 copy-start.6
  115.1 0.0 all-reduce.2.cloned.1.call-update
  115.1 133.1 %all-reduce.2.cloned.1.call-done = f32[1024,256]{0,1:T(8,128)} async-done(((f32[1024,256]{0,1:T(8,128)}), f32[1024,256]{0,1:T(8,128)}) %all-reduce.2.cloned.1.call-update) | async-done | bytes 1048592 | tf_op jit(solution)/shard_map/psum | solution.py:62
  248.2 0.0 copy-done.2
  248.2 0.0 copy-done.3
  248.2 0.0 copy-done.6
  248.2 2.8 %fusion.3 = f32[16,256]{1,0:T(8,128)} fusion(f32[16,256]{1,0:T(8,128)S(1)} %copy-done.3, f32[16,1024]{1,0:T(8,128)S(1)} %copy-done.1, f32[1024,256]{0,1:T(8,128)} %all-reduce.2.cloned.1.call-done, f32[1024]{0:T(1024)S(1)} %copy-done.6, f32[16,256]{1,0:T(8,128)S(1)} %copy-done.2), kind=kOutput, calls=%fused_computation.8 | convolution fusion | flops 50610176 | bytes 1167360 | tf_op jit(solution)/shard_map/dot_general | solution.py:63
  (2 shorter events, 0.0 us)
Async XLA Ops:
  6.5 19.4 %copy-start = (f32[256,128]{1,0:T(8,128)S(1)}, f32[256,128]{1,0:T(8,128)}, u32[]{:S(2)}) copy-start(f32[256,128]{1,0:T(8,128)} %param.7) | copy-start | bytes 393220
  6.5 0.7 copy-start.7
  6.5 10.6 %copy-start.4 = (f32[16,1024]{1,0:T(8,128)S(1)}, f32[16,1024]{1,0:T(8,128)}, u32[]{:S(2)}) copy-start(f32[16,1024]{1,0:T(8,128)} %param.10) | copy-start | bytes 196612
  6.5 67.8 %reduce-scatter.7.cloned.1.call-start = ((), (), s32[]{:S(2)}) async-start(), calls=%async_computation.4 | async-start | bytes 147456
  43.7 0.9 copy-start.5
  43.7 68.6 %reduce-scatter.5.cloned.1.call-start = ((), (), s32[]{:S(2)}) async-start(), calls=%async_computation.2 | async-start | bytes 81920 | tf_op jit(solution)/shard_map/reduce_scatter | solution.py:41
  89.9 22.4 %copy-start.1 = (f32[16,1024]{1,0:T(8,128)S(1)}, f32[16,1024]{1,0:T(8,128)}, u32[]{:S(2)}) copy-start(f32[16,1024]{1,0:T(8,128)} %param.12) | copy-start | bytes 196612
  89.9 158.3 %all-reduce.2.cloned.1.call-start = ((), (), s32[]{:S(2)}) async-start(), calls=%async_computation.3 | async-start | bytes 2097152 | tf_op jit(solution)/shard_map/psum | solution.py:62
  115.1 133.2 %copy-start.2 = (f32[16,256]{1,0:T(8,128)S(1)}, f32[16,256]{1,0:T(8,128)}, u32[]{:S(2)}) copy-start(f32[16,256]{1,0:T(8,128)} %reduce-scatter.5.cloned.1.call-done) | copy-start | bytes 49156
  115.1 133.2 %copy-start.3 = (f32[16,256]{1,0:T(8,128)S(1)}, f32[16,256]{1,0:T(8,128)}, u32[]{:S(2)}) copy-start(f32[16,256]{1,0:T(8,128)} %param.11) | copy-start | bytes 49156
  115.1 133.2 %copy-start.6 = (f32[1024]{0:T(1024)S(1)}, f32[1024]{0:T(1024)}, u32[]{:S(2)}) copy-start(f32[1024]{0:T(1024)} %param.13) | copy-start | bytes 12292
Sparse Core Ops, SparseCore 0:
  43.8 30.4 reduce-scatter.6
  90.1 22.1 reduce-scatter.4
  117.5 130.6 all-reduce.1
where the time goes:
time: 258 us
  waiting for transfers between devices  185 us (72%)
  blocking collectives  47.8 us (19%)
  between operations  13.2 us (5%)
  matrix products  8.16 us (3%)
    psum x1, waiting for transfers between devices, on_device(): coords = lax.psum(local_coords, ('batch', 'centre'))  133 us
    unnamed x4, waiting for transfers between devices  29.7 us
    reduce_scatter x1, waiting for transfers between devices, on_device(): lax.psum_scatter(lax.dot_general(kernel, residual, (((0,), (0,)), ((), ()...  22.3 us
    all_gather x1, blocking collectives, on_device(): batch_x = lax.all_gather(picked, 'centre', axis=1, tiled=True)  15.2 us
    all_gather x1, blocking collectives, on_device(): lax.all_gather(columns - own_targets, 'centre', axis=1, tiled=True)  13.9 us
    all_gather x1, blocking collectives, on_device(): crows = lax.all_gather(coeffs, 'batch', axis=0, tiled=True)  9.88 us
    all_gather x1, blocking collectives, on_device(): zrows = lax.all_gather(centres, 'batch', axis=0, tiled=True)  8.8 us
  transfers between devices with their start and end apart: 3, of which 3 were waited for; matrix products, arithmetic and copies ran while one was open for 0% of the time, Pallas kernels for 0%

commit v1 on v0

--- a/solution.py
+++ b/solution.py
@@ -59,7 +59,7 @@
         precision=highest,
         preferred_element_type=jnp.float32,
     )
-    coords = lax.psum(local_coords, ("batch", "centre"))
+    coords = jnp.sum(lax.all_gather(local_coords, ("batch", "centre")), axis=0)
     correction = jnp.dot(
         eigvecs, eigscale[:, None] * coords, precision=highest, preferred_element_type=jnp.float32
     )

time: 258 us -> 356 us (1.38)
  waiting for transfers between devices: 185 us -> 248 us
  local copies, waits for them, and re-layouts: 1.63 us -> 30.4 us
  other arithmetic: 1.54 us -> 9.72 us
    all_gather x0 -> x1, waiting for transfers between devices: none -> 196 us  [on_device(): coords = jnp.sum(lax.all_gather(local_coords, ('batch', 'centre')), axis=0)]
    psum x1 -> x0, waiting for transfers between devices: 133 us -> none  [on_device(): coords = lax.psum(local_coords, ('batch', 'centre'))]
    unnamed x17 -> x14, local copies, waits for them, and re-layouts: 0.91 us -> 28.9 us
    reduce_sum x0 -> x1, other arithmetic: none -> 7.55 us  [on_device(): coords = jnp.sum(lax.all_gather(local_coords, ('batch', 'centre')), axis=0)]
where the time goes in v1:
time: 356 us
  waiting for transfers between devices  248 us (70%)
  blocking collectives  47.8 us (13%)
  local copies, waits for them, and re-layouts  30.4 us (9%)
  between operations  13.2 us (4%)
  other arithmetic  9.72 us (3%)
  matrix products  7.03 us (2%)
    all_gather x1, waiting for transfers between devices, on_device(): coords = jnp.sum(lax.all_gather(local_coords, ('batch', 'centre')), axis=0)  196 us
    unnamed x4, waiting for transfers between devices  29.7 us
    unnamed x14, local copies, waits for them, and re-layouts  28.9 us
    reduce_scatter x1, waiting for transfers between devices, on_device(): lax.psum_scatter(lax.dot_general(kernel, residual, (((0,), (0,)), ((), ()...  22.3 us
    all_gather x1, blocking collectives, on_device(): batch_x = lax.all_gather(picked, 'centre', axis=1, tiled=True)  15.2 us
    all_gather x1, blocking collectives, on_device(): lax.all_gather(columns - own_targets, 'centre', axis=1, tiled=True)  13.9 us
    all_gather x1, blocking collectives, on_device(): crows = lax.all_gather(coeffs, 'batch', axis=0, tiled=True)  9.87 us
    all_gather x1, blocking collectives, on_device(): zrows = lax.all_gather(centres, 'batch', axis=0, tiled=True)  8.79 us
  transfers between devices with their start and end apart: 3, of which 3 were waited for; matrix products, arithmetic and copies ran while one was open for 0% of the time, Pallas kernels for 0%

profile of v1, /device:TPU:0, one launch (start us, length us, event | category | flops | bytes accessed | tf_op | source)
XLA Modules:
  0.0 355.9 jit_solution(2019846585788553945)
XLA Ops:
  6.5 0.0 copy-start
  6.5 0.0 reduce-scatter.7.cloned.1.call-start
  6.5 0.7 compare_and_fusion
  7.2 0.7 compare_select_fusion
  7.9 9.9 %all_gather.20 = f32[64,256]{1,0:T(8,128)S(1)} all-gather(f32[16,256]{1,0:T(8,128)} %param.11), channel_id=1, replica_groups=mesh['batch'=4,'centre'=8] {'batch'}, dimensions={0}, use_global_device_ids=true | all-gather | bytes 81920 | tf_op jit(solution)/shard_map/all_gather | solution.py:22
  17.8 8.8 %all_gather.19 = f32[64,1024]{1,0:T(8,128)S(1)} all-gather(f32[16,1024]{1,0:T(8,128)} %param.10), channel_id=1, replica_groups=mesh['batch'=4,'centre'=8] {'batch'}, dimensions={0}, use_global_device_ids=true | all-gather | bytes 327680 | tf_op jit(solution)/shard_map/all_gather | solution.py:21
  26.6 0.0 copy-done
  26.6 0.6 gather_fusion
  27.2 0.1 broadcast_select_fusion
  27.3 15.2 %all_gather.18 = f32[128,1024]{1,0:T(8,128)S(1)} all-gather(f32[128,128]{1,0:T(8,128)S(1)} %broadcast_select_fusion), channel_id=1, replica_groups=mesh['batch'=4,'centre'=8] {'centre'}, dimensions={1}, use_global_device_ids=true | all-gather | bytes 589824 | tf_op jit(solution)/shard_map/all_gather | solution.py:10
  42.5 0.7 fusion
  43.2 1.1 convolution_bitcast_fusion.1
  44.2 0.0 reduce-scatter.7.cloned.1.call-update
  44.3 0.0 reduce-scatter.5.cloned.1.call-start
  44.3 0.9 constant_dynamic-slice_fusion
  45.2 0.1 copy.15
  45.3 29.6 %reduce-scatter.7.cloned.1.call-done = f32[32,128]{1,0:T(8,128)} async-done(((f32[256,128]{1,0:T(8,128)}), f32[32,128]{1,0:T(8,128)}) %reduce-scatter.7.cloned.1.call-update) | async-done | bytes 16400
  74.9 0.7 fusion.6
  75.6 13.9 %all_gather.21 = f32[128,256]{0,1:T(8,128)S(1)} all-gather(f32[128,32]{0,1:T(8,128)S(1)} %fusion.6), channel_id=1, replica_groups=mesh['batch'=4,'centre'=8] {'centre'}, dimensions={1}, use_global_device_ids=true | all-gather | bytes 147456 | tf_op jit(solution)/shard_map/all_gather | solution.py:39
  89.6 0.9 fusion.10
  90.5 0.0 reduce-scatter.5.cloned.1.call-update
  90.5 0.0 all-gather.3.cloned.1.call-start
  90.6 22.3 %reduce-scatter.5.cloned.1.call-done = f32[16,256]{1,0:T(8,128)} async-done(((f32[64,256]{1,0:T(8,128)}), f32[16,256]{1,0:T(8,128)}) %reduce-scatter.5.cloned.1.call-update) | async-done | bytes 16400 | tf_op jit(solution)/shard_map/reduce_scatter | solution.py:41
  112.9 2.9 convolution_bitcast_fusion
  115.7 0.0 all-gather.3.cloned.1.call-update
  115.8 195.6 %all-gather.3.cloned.1.call-done = f32[32768,256]{0,1:T(8,128)} async-done(((f32[1024,256]{0,1:T(8,128)}), f32[32768,256]{0,1:T(8,128)}) %all-gather.3.cloned.1.call-update) | async-done | bytes 33554448 | tf_op jit(solution)/shard_map/all_gather | solution.py:62
  311.3 0.0 copy-start.1
  311.3 28.8 %copy.16 = f32[32,8,32,1024]{3,2,1,0:T(8,128)S(1)} copy(f32[32,8,32,1024]{3,1,2,0:T(8,128)} %bitcast.29) | data formatting | bytes 67108864
  340.1 0.0 copy-start.2
  340.2 0.0 copy-start.3
  340.2 0.0 copy-start.4
  340.2 0.0 copy-start.5
  340.2 7.6 %bitcast_reduce_fusion = f32[1024,256]{0,1:T(8,128)S(1)} fusion(f32[32,8,32,1024]{3,2,1,0:T(8,128)S(1)} %copy.16), kind=kLoop, calls=%fused_computation.1 | loop fusion | flops 8126464 | bytes 34603008 | tf_op jit(solution)/shard_map/reduce_sum | solution.py:62
  347.7 0.0 copy-done.2
  347.8 0.0 copy-done.3
  347.8 0.0 copy-done.4
  347.8 0.0 copy-done.5
  347.8 1.5 fusion.3
  349.3 0.0 copy-done.1
  (1 shorter events, 0.0 us)
Async XLA Ops:
  6.5 20.0 %copy-start = (f32[256,128]{1,0:T(8,128)S(1)}, f32[256,128]{1,0:T(8,128)}, u32[]{:S(2)}) copy-start(f32[256,128]{1,0:T(8,128)} %param.7) | copy-start | bytes 393220
  6.5 68.4 %reduce-scatter.7.cloned.1.call-start = ((), (), s32[]{:S(2)}) async-start(), calls=%async_computation.4 | async-start | bytes 147456
  44.3 68.6 %reduce-scatter.5.cloned.1.call-start = ((), (), s32[]{:S(2)}) async-start(), calls=%async_computation.2 | async-start | bytes 81920 | tf_op jit(solution)/shard_map/reduce_scatter | solution.py:41
  90.5 220.8 %all-gather.3.cloned.1.call-start = ((), (), s32[]{:S(2)}) async-start(), calls=%async_computation.3 | async-start | bytes 34603008 | tf_op jit(solution)/shard_map/all_gather | solution.py:62
  311.3 38.0 %copy-start.1 = (f32[256,128]{1,0:T(8,128)S(1)}, f32[256,128]{1,0:T(8,128)}, u32[]{:S(2)}) copy-start(f32[256,128]{1,0:T(8,128)} %param.7) | copy-start | bytes 393220
  340.1 7.6 %copy-start.2 = (f32[16,1024]{1,0:T(8,128)S(1)}, f32[16,1024]{1,0:T(8,128)}, u32[]{:S(2)}) copy-start(f32[16,1024]{1,0:T(8,128)} %param.12) | copy-start | bytes 196612
  340.2 7.6 %copy-start.3 = (f32[16,256]{1,0:T(8,128)S(1)}, f32[16,256]{1,0:T(8,128)}, u32[]{:S(2)}) copy-start(f32[16,256]{1,0:T(8,128)} %reduce-scatter.5.cloned.1.call-done) | copy-start | bytes 49156
  340.2 7.6 %copy-start.4 = (f32[16,256]{1,0:T(8,128)S(1)}, f32[16,256]{1,0:T(8,128)}, u32[]{:S(2)}) copy-start(f32[16,256]{1,0:T(8,128)} %param.11) | copy-start | bytes 49156
  340.2 7.6 %copy-start.5 = (f32[1024]{0:T(1024)S(1)}, f32[1024]{0:T(1024)}, u32[]{:S(2)}) copy-start(f32[1024]{0:T(1024)} %param.13) | copy-start | bytes 12292
Sparse Core Ops, SparseCore 0:
  44.4 30.4 reduce-scatter.6
  90.6 22.1 reduce-scatter.4
  115.9 195.3 all-gather.2

commit v2 on v0

--- a/solution.py
+++ b/solution.py
@@ -59,7 +59,7 @@
         precision=highest,
         preferred_element_type=jnp.float32,
     )
-    coords = lax.psum(local_coords, ("batch", "centre"))
+    coords = lax.psum(lax.psum(local_coords, "centre"), "batch")
     correction = jnp.dot(
         eigvecs, eigscale[:, None] * coords, precision=highest, preferred_element_type=jnp.float32
     )

time: 258 us -> 239 us (0.926)
  waiting for transfers between devices: 185 us -> 166 us
    psum x1 -> x2, waiting for transfers between devices: 133 us -> 114 us  [on_device(): coords = lax.psum(lax.psum(local_coords, 'centre'), 'batch')]
    unnamed x4 -> x5, waiting for transfers between devices: 29.7 us -> 29.7 us
  transfers between devices with their start and end apart: 3 -> 4, of which waited for: 3 -> 4; matrix products, arithmetic and copies ran while one was open for 0% -> 0% of each run, Pallas kernels for 0% -> 0%
where the time goes in v2:
time: 239 us; the launch traced here: 238 us
  waiting for transfers between devices  166 us (69%)
  blocking collectives  47.8 us (20%)
  between operations  13.2 us (6%)
  matrix products  8.16 us (3%)
    psum x2, waiting for transfers between devices, on_device(): coords = lax.psum(lax.psum(local_coords, 'centre'), 'batch')  114 us
    unnamed x5, waiting for transfers between devices  29.7 us
    reduce_scatter x1, waiting for transfers between devices, on_device(): lax.psum_scatter(lax.dot_general(kernel, residual, (((0,), (0,)), ((), ()...  22.3 us
    all_gather x1, blocking collectives, on_device(): batch_x = lax.all_gather(picked, 'centre', axis=1, tiled=True)  15.2 us
    all_gather x1, blocking collectives, on_device(): lax.all_gather(columns - own_targets, 'centre', axis=1, tiled=True)  13.9 us
    all_gather x1, blocking collectives, on_device(): crows = lax.all_gather(coeffs, 'batch', axis=0, tiled=True)  9.88 us
    all_gather x1, blocking collectives, on_device(): zrows = lax.all_gather(centres, 'batch', axis=0, tiled=True)  8.8 us
  transfers between devices with their start and end apart: 4, of which 4 were waited for; matrix products, arithmetic and copies ran while one was open for 0% of the time, Pallas kernels for 0%

profile of v2, /device:TPU:0, one launch (start us, length us, event | category | flops | bytes accessed | tf_op | source)
XLA Modules:
  0.0 238.3 jit_solution(14141898400161874432)
XLA Ops:
  6.5 0.0 copy-start
  6.5 0.0 copy-start.7
  6.5 0.0 copy-start.4
  6.5 0.0 reduce-scatter.7.cloned.1.call-start
  6.5 0.7 compare_and_fusion
  7.3 0.0 copy-done.7
  7.3 9.9 %all_gather.14 = f32[64,256]{1,0:T(8,128)S(1)} all-gather(f32[16,256]{1,0:T(8,128)} %param.11), channel_id=1, replica_groups=mesh['batch'=4,'centre'=8] {'batch'}, dimensions={0}, use_global_device_ids=true | all-gather | bytes 81920 | tf_op jit(solution)/shard_map/all_gather | solution.py:22
  17.2 0.0 copy-done.4
  17.2 8.8 %all_gather.13 = f32[64,1024]{1,0:T(8,128)S(1)} all-gather(f32[16,1024]{1,0:T(8,128)S(1)} %copy-done.4), channel_id=1, replica_groups=mesh['batch'=4,'centre'=8] {'batch'}, dimensions={0}, use_global_device_ids=true | all-gather | bytes 327680 | tf_op jit(solution)/shard_map/all_gather | solution.py:21
  26.0 0.0 copy-done
  26.0 0.6 gather_fusion
  26.6 0.1 broadcast_select_fusion
  26.7 15.2 %all_gather.12 = f32[128,1024]{1,0:T(8,128)S(1)} all-gather(f32[128,128]{1,0:T(8,128)S(1)} %broadcast_select_fusion), channel_id=1, replica_groups=mesh['batch'=4,'centre'=8] {'centre'}, dimensions={1}, use_global_device_ids=true | all-gather | bytes 589824 | tf_op jit(solution)/shard_map/all_gather | solution.py:10
  41.9 0.7 fusion
  42.6 1.1 convolution_bitcast_fusion.1
  43.7 0.0 copy-start.5
  43.7 0.0 reduce-scatter.7.cloned.1.call-update
  43.7 0.0 reduce-scatter.5.cloned.1.call-start
  43.7 0.8 copy-done.5
  44.6 0.1 constant_dynamic-slice_fusion
  44.6 0.1 copy.15
  44.7 29.6 %reduce-scatter.7.cloned.1.call-done = f32[32,128]{1,0:T(8,128)} async-done(((f32[256,128]{1,0:T(8,128)}), f32[32,128]{1,0:T(8,128)}) %reduce-scatter.7.cloned.1.call-update) | async-done | bytes 16400
  74.3 0.7 fusion.6
  75.1 13.9 %all_gather.15 = f32[128,256]{0,1:T(8,128)S(1)} all-gather(f32[128,32]{0,1:T(8,128)S(1)} %fusion.6), channel_id=1, replica_groups=mesh['batch'=4,'centre'=8] {'centre'}, dimensions={1}, use_global_device_ids=true | all-gather | bytes 147456 | tf_op jit(solution)/shard_map/all_gather | solution.py:39
  89.0 0.9 fusion.10
  89.9 0.0 copy-start.1
  89.9 0.0 reduce-scatter.5.cloned.1.call-update
  89.9 0.0 all-reduce.3.cloned.1.call-start
  90.0 22.3 %reduce-scatter.5.cloned.1.call-done = f32[16,256]{1,0:T(8,128)} async-done(((f32[64,256]{1,0:T(8,128)}), f32[16,256]{1,0:T(8,128)}) %reduce-scatter.5.cloned.1.call-update) | async-done | bytes 16400 | tf_op jit(solution)/shard_map/reduce_scatter | solution.py:41
  112.3 0.0 copy-done.1
  112.3 2.8 %convolution_bitcast_fusion = f32[1024,256]{0,1:T(8,128)} fusion(f32[16,1024]{1,0:T(8,128)S(1)} %copy-done.1, f32[16,256]{1,0:T(8,128)} %reduce-scatter.5.cloned.1.call-done), kind=kOutput, calls=%fused_computation.1 | convolution fusion | flops 50335744 | bytes 1130496 | tf_op jit(solution)/shard_map/dot_general | solution.py:55
  115.1 0.0 all-reduce.3.cloned.1.call-update
  115.1 0.0 all-reduce.5.cloned.1.call-start
  115.2 59.3 %all-reduce.3.cloned.1.call-done = f32[1024,256]{0,1:T(8,128)} async-done(((f32[1024,256]{0,1:T(8,128)}), f32[1024,256]{0,1:T(8,128)}) %all-reduce.3.cloned.1.call-update) | async-done | bytes 1048592 | tf_op jit(solution)/shard_map/psum | solution.py:62
  174.5 0.0 copy-start.2
  174.5 0.0 copy-start.3
  174.5 0.0 copy-start.6
  174.5 0.0 all-reduce.5.cloned.1.call-update
  174.5 54.5 %all-reduce.5.cloned.1.call-done = f32[1024,256]{0,1:T(8,128)} async-done(((f32[1024,256]{0,1:T(8,128)}), f32[1024,256]{0,1:T(8,128)}) %all-reduce.5.cloned.1.call-update) | async-done | bytes 1048592 | tf_op jit(solution)/shard_map/psum | solution.py:62
  229.0 0.0 copy-done.2
  229.0 0.0 copy-done.3
  229.0 0.0 copy-done.6
  229.0 2.8 %fusion.3 = f32[16,256]{1,0:T(8,128)} fusion(f32[16,256]{1,0:T(8,128)S(1)} %copy-done.3, f32[16,1024]{1,0:T(8,128)S(1)} %copy-done.1, f32[1024,256]{0,1:T(8,128)} %all-reduce.5.cloned.1.call-done, f32[1024]{0:T(1024)S(1)} %copy-done.6, f32[16,256]{1,0:T(8,128)S(1)} %copy-done.2), kind=kOutput, calls=%fused_computation.8 | convolution fusion | flops 50610176 | bytes 1167360 | tf_op jit(solution)/shard_map/dot_general | solution.py:63
  (2 shorter events, 0.0 us)
Async XLA Ops:
  6.5 19.4 %copy-start = (f32[256,128]{1,0:T(8,128)S(1)}, f32[256,128]{1,0:T(8,128)}, u32[]{:S(2)}) copy-start(f32[256,128]{1,0:T(8,128)} %param.7) | copy-start | bytes 393220
  6.5 0.7 copy-start.7
  6.5 10.6 %copy-start.4 = (f32[16,1024]{1,0:T(8,128)S(1)}, f32[16,1024]{1,0:T(8,128)}, u32[]{:S(2)}) copy-start(f32[16,1024]{1,0:T(8,128)} %param.10) | copy-start | bytes 196612
  6.5 67.8 %reduce-scatter.7.cloned.1.call-start = ((), (), s32[]{:S(2)}) async-start(), calls=%async_computation.5 | async-start | bytes 147456
  43.7 0.9 copy-start.5
  43.7 68.6 %reduce-scatter.5.cloned.1.call-start = ((), (), s32[]{:S(2)}) async-start(), calls=%async_computation.2 | async-start | bytes 81920 | tf_op jit(solution)/shard_map/reduce_scatter | solution.py:41
  89.9 22.4 %copy-start.1 = (f32[16,1024]{1,0:T(8,128)S(1)}, f32[16,1024]{1,0:T(8,128)}, u32[]{:S(2)}) copy-start(f32[16,1024]{1,0:T(8,128)} %param.12) | copy-start | bytes 196612
  89.9 84.5 %all-reduce.3.cloned.1.call-start = ((), (), s32[]{:S(2)}) async-start(), calls=%async_computation.3 | async-start | bytes 2097152 | tf_op jit(solution)/shard_map/psum | solution.py:62
  115.1 113.9 %all-reduce.5.cloned.1.call-start = ((), (), s32[]{:S(2)}) async-start(), calls=%async_computation.4 | async-start | bytes 2097152 | tf_op jit(solution)/shard_map/psum | solution.py:62
  174.5 54.5 %copy-start.2 = (f32[16,256]{1,0:T(8,128)S(1)}, f32[16,256]{1,0:T(8,128)}, u32[]{:S(2)}) copy-start(f32[16,256]{1,0:T(8,128)} %reduce-scatter.5.cloned.1.call-done) | copy-start | bytes 49156
  174.5 54.5 %copy-start.3 = (f32[16,256]{1,0:T(8,128)S(1)}, f32[16,256]{1,0:T(8,128)}, u32[]{:S(2)}) copy-start(f32[16,256]{1,0:T(8,128)} %param.11) | copy-start | bytes 49156
  174.5 54.5 %copy-start.6 = (f32[1024]{0:T(1024)S(1)}, f32[1024]{0:T(1024)}, u32[]{:S(2)}) copy-start(f32[1024]{0:T(1024)} %param.13) | copy-start | bytes 12292
Sparse Core Ops, SparseCore 0:
  43.8 30.4 reduce-scatter.6
  90.1 22.1 reduce-scatter.4
  115.2 59.2 all-reduce.2
  177.4 51.5 all-reduce.4
